TPU v7x, 16 devices: a whole 2x2x2 slice. The times are simulated.
16 devices in a mesh: sp: 16 (over z, y, x, core).
Axes of the slice: x: 2, y: 2, z: 2, core: 2. Of those that a mesh axis runs over, the one named last changes fastest.
Arguments:
- x_act: bfloat16 [4096, 1024], P('sp')
- positions: int32 [4096], P('sp')
- grad_out: bfloat16 [4096, 1024], P('sp')
- g_attn: bfloat16 [1024], P('sp')
- w_q: bfloat16 [1024, 16, 64], P('sp')
- w_k: bfloat16 [1024, 16, 64], P('sp')
- w_v: bfloat16 [1024, 16, 64], P('sp')
- w_o: bfloat16 [16, 64, 1024], P('sp')
- g_mlp: bfloat16 [1024], P('sp')
- w_gate: bfloat16 [1024, 2816], P('sp')
- w_up: bfloat16 [1024, 2816], P('sp')
- w_down: bfloat16 [2816, 1024], P('sp')
Outputs:
- output 1: bfloat16 [4096, 1024], P('sp')
- output 2: bfloat16 [4096, 1024], P('sp')
- output 3: float32 [1024], P('sp')
- output 4: float32 [1024, 16, 64], P('sp')
- output 5: float32 [1024, 16, 64], P('sp')
- output 6: float32 [1024, 16, 64], P('sp')
- output 7: float32 [16, 64, 1024], P('sp')
- output 8: float32 [1024], P('sp')
- output 9: float32 [1024, 2816], P('sp')
- output 10: float32 [1024, 2816], P('sp')
- output 11: float32 [2816, 1024], P('sp')
All inputs are finite; a program needn't handle non-finite values.
Results may differ from a plain program's by a relative error of at most 0.0169985.
Values are sent between devices in bfloat16 or wider.
A program may use at most 1 GiB of HBM per device.

v0:
```python
import jax
import jax.numpy as jnp
from jax import lax
from jax.sharding import PartitionSpec as P

SEQ_AXIS = 'sp'
RMS_EPS = 1e-5
ROPE_BASE = 10000.0
MASK_VALUE = -1e30


def rms_norm(act_in, gain_vec):
    act_f = act_in.astype(jnp.float32)
    inv_rms = lax.rsqrt(jnp.mean(act_f * act_f, axis=-1, keepdims=True) + RMS_EPS)
    return (act_f * inv_rms * gain_vec.astype(jnp.float32)).astype(jnp.bfloat16), inv_rms


def rms_norm_bwd(act_in, gain_vec, inv_rms, d_normed):
    act_f = act_in.astype(jnp.float32)
    d_f = d_normed.astype(jnp.float32)
    scaled_d = d_f * gain_vec.astype(jnp.float32)
    proj_mean = jnp.mean(scaled_d * act_f, axis=-1, keepdims=True)
    d_act = inv_rms * scaled_d - act_f * (inv_rms * inv_rms * inv_rms) * proj_mean
    d_gain = jnp.sum(d_f * act_f * inv_rms, axis=0)
    return d_act, d_gain


def rope_tables(positions, head_dim):
    half_dim = head_dim // 2
    inv_freq = ROPE_BASE ** (-(jnp.arange(half_dim, dtype=jnp.float32) * (2.0 / head_dim)))
    angle_tab = positions.astype(jnp.float32)[:, None] * inv_freq[None, :]
    return jnp.cos(angle_tab)[:, None, :], jnp.sin(angle_tab)[:, None, :]


def apply_rope(values_in, cos_tab, sin_tab):
    half_dim = values_in.shape[-1] // 2
    first_half = values_in[..., :half_dim]
    second_half = values_in[..., half_dim:]
    return jnp.concatenate([first_half * cos_tab - second_half * sin_tab, second_half * cos_tab + first_half * sin_tab], axis=-1)


def dot_tn(lhs_mat, rhs_mat):
    return lax.dot_general(lhs_mat, rhs_mat, (((0,), (0,)), ((), ())), preferred_element_type=jnp.float32)


def dot_nt(lhs_mat, rhs_mat):
    return lax.dot_general(lhs_mat, rhs_mat, (((1,), (1,)), ((), ())), preferred_element_type=jnp.float32)


def project_qkv(x_act, positions, g_attn, w_q, w_k, w_v):
    cos_tab, sin_tab = rope_tables(positions, w_q.shape[2])
    normed, inv_rms = rms_norm(x_act, g_attn)
    q_proj = apply_rope(jnp.einsum('td,dhe->the', normed, w_q, preferred_element_type=jnp.float32), cos_tab, sin_tab).astype(jnp.bfloat16)
    k_proj = apply_rope(jnp.einsum('td,dhe->the', normed, w_k, preferred_element_type=jnp.float32), cos_tab, sin_tab).astype(jnp.bfloat16)
    v_proj = jnp.einsum('td,dhe->the', normed, w_v, preferred_element_type=jnp.float32).astype(jnp.bfloat16)
    return normed, inv_rms, cos_tab, sin_tab, q_proj, k_proj, v_proj


def attention_fwd(q_all, k_all, v_all, q_start):
    n_query, n_heads, head_dim = q_all.shape
    n_keys = k_all.shape[0]
    n_kv = k_all.shape[1]
    q_group = q_all.reshape(n_query, n_kv, n_heads // n_kv, head_dim)
    scores = jnp.einsum('skgd,tkd->kgst', q_group, k_all, preferred_element_type=jnp.float32) * (head_dim ** -0.5)
    causal = (q_start + jnp.arange(n_query))[:, None] >= jnp.arange(n_keys)[None, :]
    attn_prob = jax.nn.softmax(jnp.where(causal, scores, MASK_VALUE), axis=-1)
    attn_out = jnp.einsum('kgst,tkd->skgd', attn_prob.astype(jnp.bfloat16), v_all, preferred_element_type=jnp.float32)
    return attn_out.astype(jnp.bfloat16).reshape(n_query, n_heads, head_dim), attn_prob


def attention_bwd(q_all, k_all, v_all, attn_prob, d_attn):
    n_query, n_heads, head_dim = q_all.shape
    n_kv = k_all.shape[1]
    group_size = n_heads // n_kv
    q_group = q_all.reshape(n_query, n_kv, group_size, head_dim)
    d_group = d_attn.reshape(n_query, n_kv, group_size, head_dim)
    d_v = jnp.einsum('kgst,skgd->tkd', attn_prob.astype(jnp.bfloat16), d_group, preferred_element_type=jnp.float32)
    d_prob = jnp.einsum('skgd,tkd->kgst', d_group, v_all, preferred_element_type=jnp.float32).astype(jnp.bfloat16).astype(jnp.float32)
    d_scores = attn_prob * (d_prob - jnp.sum(d_prob * attn_prob, axis=-1, keepdims=True))
    d_scores = (d_scores * (head_dim ** -0.5)).astype(jnp.bfloat16)
    d_q = jnp.einsum('kgst,tkd->skgd', d_scores, k_all, preferred_element_type=jnp.float32).reshape(n_query, n_heads, head_dim)
    d_k = jnp.einsum('kgst,skgd->tkd', d_scores, q_group, preferred_element_type=jnp.float32)
    return d_q, d_k, d_v


def mlp_forward(x_act, attn_loc, w_o, g_mlp, w_gate, w_up, w_down):
    hidden = (x_act.astype(jnp.float32) + jnp.einsum('the,hed->td', attn_loc, w_o, preferred_element_type=jnp.float32)).astype(jnp.bfloat16)
    normed_mlp, inv_rms_mlp = rms_norm(hidden, g_mlp)
    gate_pre = jnp.dot(normed_mlp, w_gate, preferred_element_type=jnp.float32)
    up_pre = jnp.dot(normed_mlp, w_up, preferred_element_type=jnp.float32)
    mixed_act = (jax.nn.silu(gate_pre) * up_pre).astype(jnp.bfloat16)
    y_out = (hidden.astype(jnp.float32) + jnp.dot(mixed_act, w_down, preferred_element_type=jnp.float32)).astype(jnp.bfloat16)
    return y_out, (hidden, normed_mlp, inv_rms_mlp, gate_pre, up_pre, mixed_act)


def mlp_backward(grad_out, mlp_saved, g_mlp, w_gate, w_up, w_down):
    hidden, normed_mlp, inv_rms_mlp, gate_pre, up_pre, mixed_act = mlp_saved
    grad_w_down = dot_tn(mixed_act, grad_out)
    d_mixed = dot_nt(grad_out, w_down).astype(jnp.bfloat16).astype(jnp.float32)
    gate_sig = jax.nn.sigmoid(gate_pre)
    d_up = (d_mixed * gate_pre * gate_sig).astype(jnp.bfloat16)
    d_gate = (d_mixed * up_pre * gate_sig * (1.0 + gate_pre * (1.0 - gate_sig))).astype(jnp.bfloat16)
    grad_w_gate = dot_tn(normed_mlp, d_gate)
    grad_w_up = dot_tn(normed_mlp, d_up)
    d_normed = (dot_nt(d_gate, w_gate) + dot_nt(d_up, w_up)).astype(jnp.bfloat16)
    d_hid_norm, grad_g_mlp = rms_norm_bwd(hidden, g_mlp, inv_rms_mlp, d_normed)
    d_hidden = (grad_out.astype(jnp.float32) + d_hid_norm).astype(jnp.bfloat16)
    return d_hidden, grad_g_mlp, grad_w_gate, grad_w_up, grad_w_down


def qkv_backward(x_act, normed, inv_rms, cos_tab, sin_tab, g_attn, w_q, w_k, w_v, d_q, d_k, d_v):
    d_q_raw = apply_rope(d_q.astype(jnp.float32), cos_tab, -sin_tab).astype(jnp.bfloat16)
    d_k_raw = apply_rope(d_k.astype(jnp.float32), cos_tab, -sin_tab).astype(jnp.bfloat16)
    grad_w_q = jnp.einsum('td,the->dhe', normed, d_q_raw, preferred_element_type=jnp.float32)
    grad_w_k = jnp.einsum('td,the->dhe', normed, d_k_raw, preferred_element_type=jnp.float32)
    grad_w_v = jnp.einsum('td,the->dhe', normed, d_v, preferred_element_type=jnp.float32)
    d_normed = (jnp.einsum('the,dhe->td', d_q_raw, w_q, preferred_element_type=jnp.float32) + jnp.einsum('the,dhe->td', d_k_raw, w_k, preferred_element_type=jnp.float32) + jnp.einsum('the,dhe->td', d_v, w_v, preferred_element_type=jnp.float32)).astype(jnp.bfloat16)
    d_x_norm, grad_g_attn = rms_norm_bwd(x_act, g_attn, inv_rms, d_normed)
    return d_x_norm, grad_g_attn, grad_w_q, grad_w_k, grad_w_v


def gather_weights(weight_shards):
    return tuple(lax.all_gather(shard_part, SEQ_AXIS, axis=0, tiled=True) for shard_part in weight_shards)


def layer_forward(x_act, positions, weights):
    g_attn, w_q, w_k, w_v, w_o, g_mlp, w_gate, w_up, w_down = weights
    normed, inv_rms, cos_tab, sin_tab, q_proj, k_proj, v_proj = project_qkv(x_act, positions, g_attn, w_q, w_k, w_v)
    q_seq = lax.all_to_all(q_proj, SEQ_AXIS, 1, 0, tiled=True)
    k_seq = lax.all_to_all(k_proj, SEQ_AXIS, 1, 0, tiled=True)
    v_seq = lax.all_to_all(v_proj, SEQ_AXIS, 1, 0, tiled=True)
    attn_seq, attn_prob = attention_fwd(q_seq, k_seq, v_seq, 0)
    attn_loc = lax.all_to_all(attn_seq, SEQ_AXIS, 0, 1, tiled=True)
    y_out, mlp_saved = mlp_forward(x_act, attn_loc, w_o, g_mlp, w_gate, w_up, w_down)
    attn_saved = (normed, inv_rms, cos_tab, sin_tab, q_seq, k_seq, v_seq, attn_prob, attn_loc)
    return y_out, attn_saved, mlp_saved


def device_step(x_act, positions, grad_out, *weight_shards):
    y_first = layer_forward(x_act, positions, gather_weights(weight_shards))[0]
    x_again, pos_again, shards_again, y_out = lax.optimization_barrier((x_act, positions, weight_shards, y_first))
    weights = gather_weights(shards_again)
    g_attn, w_q, w_k, w_v, w_o, g_mlp, w_gate, w_up, w_down = weights
    unused_out, attn_saved, mlp_saved = layer_forward(x_again, pos_again, weights)
    normed, inv_rms, cos_tab, sin_tab, q_seq, k_seq, v_seq, attn_prob, attn_loc = attn_saved
    d_hidden, grad_g_mlp, grad_w_gate, grad_w_up, grad_w_down = mlp_backward(grad_out, mlp_saved, g_mlp, w_gate, w_up, w_down)
    grad_w_o = jnp.einsum('the,td->hed', attn_loc, d_hidden, preferred_element_type=jnp.float32)
    d_attn_loc = jnp.einsum('td,hed->the', d_hidden, w_o, preferred_element_type=jnp.float32).astype(jnp.bfloat16)
    d_attn_seq = lax.all_to_all(d_attn_loc, SEQ_AXIS, 1, 0, tiled=True)
    d_q_seq, d_k_seq, d_v_seq = attention_bwd(q_seq, k_seq, v_seq, attn_prob, d_attn_seq)
    d_q = lax.all_to_all(d_q_seq.astype(jnp.bfloat16), SEQ_AXIS, 0, 1, tiled=True)
    d_k = lax.all_to_all(d_k_seq.astype(jnp.bfloat16), SEQ_AXIS, 0, 1, tiled=True)
    d_v = lax.all_to_all(d_v_seq.astype(jnp.bfloat16), SEQ_AXIS, 0, 1, tiled=True)
    d_x_norm, grad_g_attn, grad_w_q, grad_w_k, grad_w_v = qkv_backward(x_again, normed, inv_rms, cos_tab, sin_tab, g_attn, w_q, w_k, w_v, d_q, d_k, d_v)
    grad_x = (d_hidden.astype(jnp.float32) + d_x_norm).astype(jnp.bfloat16)
    full_grads = (grad_g_attn, grad_w_q, grad_w_k, grad_w_v, grad_w_o, grad_g_mlp, grad_w_gate, grad_w_up, grad_w_down)
    grad_shards = tuple(lax.psum_scatter(full_grad, SEQ_AXIS, scatter_dimension=0, tiled=True) for full_grad in full_grads)
    return (y_out, grad_x) + grad_shards


def solution(mesh):
    token_spec = P(SEQ_AXIS, None)
    matrix_spec = P(SEQ_AXIS, None)
    cube_spec = P(SEQ_AXIS, None, None)
    gain_spec = P(SEQ_AXIS)
    weight_specs = (gain_spec, cube_spec, cube_spec, cube_spec, cube_spec, gain_spec, matrix_spec, matrix_spec, matrix_spec)
    return jax.shard_map(device_step, mesh=mesh, in_specs=(token_spec, gain_spec, token_spec) + weight_specs, out_specs=(token_spec, token_spec) + weight_specs, check_vma=False)
```

profile of v0, /device:TPU:0, one launch (start us, length us, event | category | flops | bytes accessed | tf_op | source)
XLA Modules:
  0.0 1448.3 jit_solution(1259018588367070817)
XLA Ops:
  13.5 35.2 %all-reduce.8 = (bf16[1024]{0:T(1024)(128)(2,1)S(1)}, bf16[1024]{0:T(1024)(128)(2,1)}) all-reduce(bf16[1024]{0:T(1024)(128)(2,1)S(1)} %dynamic-update-slice, bf16[1024]{0:T(1024)(128)(2,1)S(1)} %dynamic-update-slice.1), channel_id=1, replica_groups=mesh['sp'=16] {'sp'}, use_global_device_ids=true, to_apply=%add | all-reduce | flops 2048 | bytes 8192
  59.7 27.5 %all-gather.19.cloned.1.call-done = bf16[1024,16,64]{2,1,0:T(8,128)(2,1)} async-done(((bf16[64,16,64]{2,1,0:T(8,128)(2,1)}), bf16[1024,16,64]{2,1,0:T(8,128)(2,1)}) %all-gather.19.cloned.1.call-update) | async-done | bytes 2097168 | tf_op jit(solution)/shard_map/all_gather | solution.py:123
  91.6 32.8 %all-gather.17.cloned.1.call-done = bf16[1024,16,64]{2,1,0:T(8,128)(2,1)} async-done(((bf16[64,16,64]{2,1,0:T(8,128)(2,1)}), bf16[1024,16,64]{2,1,0:T(8,128)(2,1)}) %all-gather.17.cloned.1.call-update) | async-done | bytes 2097168 | tf_op jit(solution)/shard_map/all_gather | solution.py:123
  164.4 24.2 %fusion.9 = (f32[4096]{0:T(1024)S(1)}, f32[4096,4096]{1,0:T(8,128)}) fusion(bf16[4096,64]{0,1:T(8,128)(2,1)S(1)} %bitcast.357, bf16[4096,64]{0,1:T(8,128)(2,1)S(1)} %bitcast.355), kind=kOutput, calls=%fused_computation.16 | convolution fusion | flops 2214588416 | bytes 68173824 | tf_op jit(solution)/shard_map/skgd,tkd->kgst/dot_general | solution.py:64
  188.7 21.7 %fusion.6 = f32[4096]{0:T(1024)S(1)} fusion(f32[4096,4096]{1,0:T(8,128)} %get-tuple-element.119, f32[4096]{0:T(1024)S(1)} %get-tuple-element.118), kind=kLoop, calls=%fused_computation.13 | loop fusion | flops 83881984 | bytes 67141632 | tf_op jit(solution)/shard_map/reduce_sum | solution.py:66
  210.4 27.3 %fusion.28 = bf16[4096,1,64]{0,2,1:T(8,128)(2,1)S(1)} fusion(bf16[4096,64]{0,1:T(8,128)(2,1)S(1)} %bitcast.354, f32[4096]{0:T(1024)S(1)} %fusion.6, f32[4096]{0:T(1024)S(1)} %get-tuple-element.118, f32[4096,4096]{1,0:T(8,128)} %get-tuple-element.119), kind=kOutput, calls=%fused_computation.32 | convolution fusion | flops 2248409088 | bytes 68190208 | tf_op jit(solution)/shard_map/kgst,tkd->skgd/dot_general | solution.py:67
  266.9 24.1 %all-gather.27.cloned.1.call-done = bf16[2816,1024]{1,0:T(8,128)(2,1)} async-done(((bf16[176,1024]{1,0:T(8,128)(2,1)}), bf16[2816,1024]{1,0:T(8,128)(2,1)}) %all-gather.27.cloned.1.call-update) | async-done | bytes 5767184 | tf_op jit(solution)/shard_map/all_gather | solution.py:123
  304.2 32.4 %all-reduce.7 = (bf16[1024]{0:T(1024)(128)(2,1)S(1)}, bf16[1024]{0:T(1024)(128)(2,1)}) all-reduce(bf16[1024]{0:T(1024)(128)(2,1)S(1)} %dynamic-update-slice.2, bf16[1024]{0:T(1024)(128)(2,1)S(1)} %dynamic-update-slice.3), channel_id=1, replica_groups=mesh['sp'=16] {'sp'}, use_global_device_ids=true, to_apply=%add.2 | all-reduce | flops 2048 | bytes 8192
  343.7 30.2 %all-gather.33.cloned.1.call-done = bf16[1024,16,64]{2,1,0:T(8,128)(2,1)} async-done(((bf16[64,16,64]{2,1,0:T(8,128)(2,1)}), bf16[1024,16,64]{2,1,0:T(8,128)(2,1)}) %all-gather.33.cloned.1.call-update) | async-done | bytes 2097168 | tf_op jit(solution)/shard_map/all_gather | solution.py:123
  403.4 16.2 %all-gather.29.cloned.1.call-done = bf16[1024,16,64]{2,1,0:T(8,128)(2,1)} async-done(((bf16[64,16,64]{2,1,0:T(8,128)(2,1)}), bf16[1024,16,64]{2,1,0:T(8,128)(2,1)}) %all-gather.29.cloned.1.call-update) | async-done | bytes 2097168 | tf_op jit(solution)/shard_map/all_gather | solution.py:123
  439.3 24.2 %fusion.10 = (f32[4096]{0:T(1024)S(1)}, f32[4096,4096]{1,0:T(8,128)}) fusion(bf16[4096,64]{0,1:T(8,128)(2,1)S(1)} %bitcast.335, bf16[4096,64]{0,1:T(8,128)(2,1)S(1)} %bitcast.337), kind=kOutput, calls=%fused_computation.17 | convolution fusion | flops 2214588416 | bytes 68173824 | tf_op jit(solution)/shard_map/skgd,tkd->kgst/dot_general | solution.py:64
  463.5 21.7 %fusion.8 = f32[4096]{0:T(1024)S(1)} fusion(f32[4096,4096]{1,0:T(8,128)} %get-tuple-element.123, f32[4096]{0:T(1024)S(1)} %get-tuple-element.122), kind=kLoop, calls=%fused_computation.15 | loop fusion | flops 83881984 | bytes 67141632 | tf_op jit(solution)/shard_map/reduce_sum | solution.py:66
  485.3 27.4 %fusion.35 = bf16[4096,1,64]{0,2,1:T(8,128)(2,1)S(1)} fusion(bf16[4096,64]{0,1:T(8,128)(2,1)S(1)} %bitcast.350, f32[4096]{0:T(1024)S(1)} %fusion.8, f32[4096]{0:T(1024)S(1)} %get-tuple-element.122, f32[4096,4096]{1,0:T(8,128)} %get-tuple-element.123), kind=kOutput, calls=%fused_computation.35 | convolution fusion | flops 2248409088 | bytes 68190208 | tf_op jit(solution)/shard_map/kgst,tkd->skgd/dot_general | solution.py:67
  549.4 31.6 %all-gather.37.cloned.1.call-done = bf16[2816,1024]{1,0:T(8,128)(2,1)} async-done(((bf16[176,1024]{1,0:T(8,128)(2,1)}), bf16[2816,1024]{1,0:T(8,128)(2,1)}) %all-gather.37.cloned.1.call-update) | async-done | bytes 5767184 | tf_op jit(solution)/shard_map/all_gather | solution.py:123
  611.6 28.1 %fusion.32 = bf16[4096,1,64]{0,2,1:T(8,128)(2,1)S(1)} fusion(bf16[4096,64]{0,1:T(8,128)(2,1)S(1)} %bitcast.352, f32[4096]{0:T(1024)S(1)} %fusion.8, f32[4096]{0:T(1024)S(1)} %get-tuple-element.122, f32[4096,4096]{1,0:T(8,128)} %get-tuple-element.123), kind=kOutput, calls=%fused_computation.34 | convolution fusion | flops 2248409088 | bytes 68190208 | tf_op jit(solution)/shard_map/kgst,skgd->tkd/dot_general | solution.py:77
  645.2 40.3 %fusion.2 = (f32[4096]{0:T(1024)S(1)}, bf16[4096,4096]{1,0:T(8,128)(2,1)}) fusion(f32[4096]{0:T(1024)S(1)} %fusion.8, f32[4096]{0:T(1024)S(1)} %get-tuple-element.122, f32[4096,4096]{1,0:T(8,128)} %get-tuple-element.123, bf16[4096,64]{0,1:T(8,128)(2,1)S(1)} %bitcast.351, bf16[4096,64]{0,1:T(8,128)(2,1)S(1)} %bitcast.353), kind=kOutput, calls=%fused_computation.5 | convolution fusion | flops 2298474496 | bytes 101761024 | tf_op jit(solution)/shard_map/skgd,tkd->kgst/dot_general | solution.py:78
  694.8 44.3 %fusion.11 = bf16[4096,4096]{0,1:T(8,128)(2,1)} fusion(bf16[4096,4096]{1,0:T(8,128)(2,1)} %get-tuple-element.128, f32[4096]{0:T(1024)S(1)} %get-tuple-element.127, f32[4096]{0:T(1024)S(1)} %fusion.8, f32[4096]{0:T(1024)S(1)} %get-tuple-element.122, f32[4096,4096]{1,0:T(8,128)} %get-tuple-element.123), kind=kLoop, calls=%fused_computation.18 | loop fusion | flops 167772160 | bytes 134266880 | tf_op jit(solution)/shard_map/reshape.42
  759.8 15.5 %fusion.38 = bf16[4096,1,64]{0,2,1:T(8,128)(2,1)S(1)} fusion(bf16[4096,64]{0,1:T(8,128)(2,1)S(1)} %bitcast.338, bf16[4096,4096]{0,1:T(8,128)(2,1)} %fusion.11), kind=kOutput, calls=%fused_computation.36 | convolution fusion | flops 2147745792 | bytes 34603008 | tf_op jit(solution)/shard_map/kgst,skgd->tkd/dot_general | solution.py:82
  858.1 31.7 %all-reduce.6 = (f32[1024]{0:T(1024)S(1)}, f32[1024]{0:T(1024)S(1)}) all-reduce(f32[1024]{0:T(1024)S(1)} %get-tuple-element.81, f32[1024]{0:T(1024)S(1)} %copy-done.45), channel_id=2, replica_groups=mesh['sp'=16] {'sp'}, use_global_device_ids=true, to_apply=%region_12.13.clone | all-reduce | flops 2048 | bytes 16384
  907.6 91.0 %reduce-scatter.10.cloned.1.call-done = f32[64,16,64]{2,0,1:T(8,128)} async-done(((f32[1024,16,64]{2,0,1:T(8,128)}), f32[64,16,64]{2,0,1:T(8,128)}) %reduce-scatter.10.cloned.1.call-update) | async-done | bytes 262160 | tf_op jit(solution)/shard_map/reduce_scatter | solution.py:157
  1000.7 62.6 %reduce-scatter.14.cloned.1.call-done = f32[1,64,1024]{2,1,0:T(8,128)} async-done(((f32[16,64,1024]{2,1,0:T(8,128)}), f32[1,64,1024]{2,1,0:T(8,128)}) %reduce-scatter.14.cloned.1.call-update) | async-done | bytes 262160 | tf_op jit(solution)/shard_map/reduce_scatter | solution.py:157
  1063.3 126.8 %reduce-scatter.20.cloned.1.call-done = f32[176,1024]{1,0:T(8,128)} async-done(((f32[2816,1024]{1,0:T(8,128)}), f32[176,1024]{1,0:T(8,128)}) %reduce-scatter.20.cloned.1.call-update) | async-done | bytes 720912 | tf_op jit(solution)/shard_map/reduce_scatter | solution.py:157
  1190.1 125.4 %reduce-scatter.18.cloned.1.call-done = f32[64,2816]{1,0:T(8,128)} async-done(((f32[1024,2816]{1,0:T(8,128)}), f32[64,2816]{1,0:T(8,128)}) %reduce-scatter.18.cloned.1.call-update) | async-done | bytes 720912 | tf_op jit(solution)/shard_map/reduce_scatter | solution.py:157
  1315.5 125.6 %reduce-scatter.16.cloned.1.call-done = f32[64,2816]{1,0:T(8,128)} async-done(((f32[1024,2816]{1,0:T(8,128)}), f32[64,2816]{1,0:T(8,128)}) %reduce-scatter.16.cloned.1.call-update) | async-done | bytes 720912 | tf_op jit(solution)/shard_map/reduce_scatter | solution.py:157
  (302 shorter events, 364.6 us)
Async XLA Ops:
  7.2 43.0 %all-gather.15.cloned.1.call-start = ((), (), s32[]{:S(2)}) async-start(), calls=%async_computation.19 | async-start | bytes 4456448 | tf_op jit(solution)/shard_map/all_gather | solution.py:123
  7.9 79.2 %all-gather.19.cloned.1.call-start = ((), (), s32[]{:S(2)}) async-start(), calls=%async_computation.21 | async-start | bytes 4456448 | tf_op jit(solution)/shard_map/all_gather | solution.py:123
  8.7 115.8 %all-gather.17.cloned.1.call-start = ((), (), s32[]{:S(2)}) async-start(), calls=%async_computation.20 | async-start | bytes 4456448 | tf_op jit(solution)/shard_map/all_gather | solution.py:123
  9.4 248.3 %all-gather.21.cloned.1.call-start = ((), (), s32[]{:S(2)}) async-start(), calls=%async_computation.22 | async-start | bytes 2228224 | tf_op jit(solution)/shard_map/all_gather | solution.py:123
  10.0 250.9 %all-gather.23.cloned.1.call-start = ((), (), s32[]{:S(2)}) async-start(), calls=%async_computation.23 | async-start | bytes 6127616 | tf_op jit(solution)/shard_map/all_gather | solution.py:123
  10.6 256.3 %all-gather.25.cloned.1.call-start = ((), (), s32[]{:S(2)}) async-start(), calls=%async_computation.24 | async-start | bytes 6127616 | tf_op jit(solution)/shard_map/all_gather | solution.py:123
  56.4 78.0 %all-to-all-start = ((bf16[256,16,64]{0,2,1:T(8,128)(2,1)}), bf16[256,16,64]{0,2,1:T(8,128)(2,1)S(1)}, u32[]{:S(2)}, u32[]{:S(2)}) async-start(bf16[256,16,64]{0,2,1:T(8,128)(2,1)} %convert_element_type.226), calls=%async_computation | async-start | bytes 1048576 | tf_op jit(solution)/shard_map/all_to_all | solution.py:131
  151.3 139.6 %all-gather.27.cloned.1.call-start = ((), (), s32[]{:S(2)}) async-start(), calls=%async_computation.25 | async-start | bytes 6127616 | tf_op jit(solution)/shard_map/all_gather | solution.py:123
  243.6 94.5 %all-gather.31.cloned.1.call-start = ((), (), s32[]{:S(2)}) async-start(), calls=%async_computation.27 | async-start | bytes 4456448 | tf_op jit(solution)/shard_map/all_gather | solution.py:123
  300.3 73.6 %all-gather.33.cloned.1.call-start = ((), (), s32[]{:S(2)}) async-start(), calls=%async_computation.28 | async-start | bytes 4456448 | tf_op jit(solution)/shard_map/all_gather | solution.py:123
  301.0 118.6 %all-gather.29.cloned.1.call-start = ((), (), s32[]{:S(2)}) async-start(), calls=%async_computation.26 | async-start | bytes 4456448 | tf_op jit(solution)/shard_map/all_gather | solution.py:123
  301.6 232.9 %all-gather.35.cloned.1.call-start = ((), (), s32[]{:S(2)}) async-start(), calls=%async_computation.29 | async-start | bytes 2228224 | tf_op jit(solution)/shard_map/all_gather | solution.py:123
  302.3 235.5 %all-gather.41.cloned.1.call-start = ((), (), s32[]{:S(2)}) async-start(), calls=%async_computation.32 | async-start | bytes 6127616 | tf_op jit(solution)/shard_map/all_gather | solution.py:123
  302.9 239.5 %all-gather.39.cloned.1.call-start = ((), (), s32[]{:S(2)}) async-start(), calls=%async_computation.31 | async-start | bytes 6127616 | tf_op jit(solution)/shard_map/all_gather | solution.py:123
  400.4 25.4 %all-to-all-start.5 = ((bf16[256,16,64]{0,2,1:T(8,128)(2,1)}), bf16[256,16,64]{0,2,1:T(8,128)(2,1)}, u32[]{:S(2)}, u32[]{:S(2)}) async-start(bf16[256,16,64]{0,2,1:T(8,128)(2,1)} %pad_maximum_fusion.2), calls=%async_computation.5 | async-start | bytes 1048576 | tf_op jit(solution)/shard_map/all_to_all | solution.py:130
  428.4 152.6 %all-gather.37.cloned.1.call-start = ((), (), s32[]{:S(2)}) async-start(), calls=%async_computation.30 | async-start | bytes 6127616 | tf_op jit(solution)/shard_map/all_gather | solution.py:123
  642.6 42.9 %all-to-all-start.11 = ((bf16[16,2,8192]{2,1,0:T(2,128)(2,1)}), bf16[16,2,8192]{2,1,0:T(2,128)(2,1)S(1)}, u32[]{:S(2)}, u32[]{:S(2)}) async-start(bf16[16,2,8192]{2,1,0:T(2,128)(2,1)} %reshape.389), calls=%async_computation.11 | async-start | bytes 1048576 | tf_op jit(solution)/shard_map/all_to_all | solution.py:153
  645.0 248.3 %reduce-scatter.12.cloned.1.call-start = ((), (), s32[]{:S(2)}) async-start(), calls=%async_computation.35 | async-start | bytes 8912896 | tf_op jit(solution)/shard_map/reduce_scatter | solution.py:157
  782.3 123.1 %reduce-scatter.8.cloned.1.call-start = ((), (), s32[]{:S(2)}) async-start(), calls=%async_computation.33 | async-start | bytes 8912896 | tf_op jit(solution)/shard_map/reduce_scatter | solution.py:157
  812.6 186.0 %reduce-scatter.10.cloned.1.call-start = ((), (), s32[]{:S(2)}) async-start(), calls=%async_computation.34 | async-start | bytes 8912896 | tf_op jit(solution)/shard_map/reduce_scatter | solution.py:157
  817.4 245.9 %reduce-scatter.14.cloned.1.call-start = ((), (), s32[]{:S(2)}) async-start(), calls=%async_computation.36 | async-start | bytes 4456448 | tf_op jit(solution)/shard_map/reduce_scatter | solution.py:157
  821.5 368.6 %reduce-scatter.20.cloned.1.call-start = ((), (), s32[]{:S(2)}) async-start(), calls=%async_computation.39 | async-start | bytes 12255232 | tf_op jit(solution)/shard_map/reduce_scatter | solution.py:157
  829.6 485.9 %reduce-scatter.18.cloned.1.call-start = ((), (), s32[]{:S(2)}) async-start(), calls=%async_computation.38 | async-start | bytes 12255232 | tf_op jit(solution)/shard_map/reduce_scatter | solution.py:157
  837.1 604.0 %reduce-scatter.16.cloned.1.call-start = ((), (), s32[]{:S(2)}) async-start(), calls=%async_computation.37 | async-start | bytes 12255232 | tf_op jit(solution)/shard_map/reduce_scatter | solution.py:157
  (64 other events, 1367.4 us)
Sparse Core Ops, SparseCore 0:
  10.2 38.6 all-gather.14
  51.2 35.8 all-gather.18
  89.4 34.9 all-gather.16
  126.5 36.5 all-gather.20
  165.3 40.7 all-gather.22
  208.1 40.3 all-gather.24
  250.7 40.1 all-gather.26
  300.4 36.0 all-gather.30
  338.8 35.0 all-gather.32
  375.9 43.6 all-gather.28
  421.9 30.4 all-gather.34
  454.5 40.1 all-gather.40
  496.9 41.8 all-gather.38
  540.9 40.0 all-gather.36
  694.9 105.4 reduce-scatter.11
  812.7 92.7 reduce-scatter.7
  907.6 90.9 reduce-scatter.9
  1001.3 62.0 reduce-scatter.13
  1066.2 123.8 reduce-scatter.19
  1192.8 122.6 reduce-scatter.17
  1318.3 122.6 reduce-scatter.15
where the time goes:
time: 1460 us; the launch traced here: 1450 us
  waiting for transfers between devices  790 us (54%)
  matrix products  302 us (21%)
  blocking collectives  113 us (8%)
  other arithmetic  108 us (7%)
  local copies, waits for them, and re-layouts  85.9 us (6%)
  starting transfers between devices  33.3 us (2%)
  between operations  16 us (1%)
    reduce_scatter x7, waiting for transfers between devices, device_step(): lax.psum_scatter(full_grad, SEQ_AXIS, scatter_dimension=0, tiled=True)  541 us
    all_gather x14, waiting for transfers between devices, gather_weights(): lax.all_gather(shard_part, SEQ_AXIS, axis=0, tiled=True)  163 us
    unnamed x3, blocking collectives  99.3 us
    dot_general x2, matrix products, attention_fwd(): jnp.einsum('kgst,tkd->skgd', attn_prob.astype(jnp.bfloat16), v_all, prefe...  54.7 us
    dot_general x2, matrix products, attention_fwd(): jnp.einsum('skgd,tkd->kgst', q_group, k_all, preferred_element_type=jnp.f...  48.5 us
    another operation x4, other arithmetic  46 us
    reduce_sum x2, other arithmetic, attention_fwd(): attn_prob = jax.nn.softmax(jnp.where(causal, scores, MASK_VALUE), axis=-1)  43.5 us
    dot_general x1, matrix products, attention_bwd(): jnp.einsum('skgd,tkd->kgst', d_group, v_all, preferred_element_type=jnp.f...  40.3 us
  transfers between devices with their start and end apart: 32, of which 19 were waited for; matrix products, arithmetic and copies ran while one was open for 29% of the time, Pallas kernels for 0%

commit v1 on v0

v1 whole, which is shorter than its diff:
```python
import jax
import jax.numpy as jnp
from jax import lax
from jax.experimental import pallas as pl
from jax.experimental.pallas import tpu as pltpu
from jax.sharding import PartitionSpec as P

SEQ_AXIS = 'sp'
RMS_EPS = 1e-5
ROPE_BASE = 10000.0
MASK_VALUE = -1e30
TILE = 512
F32 = jnp.float32
BF16 = jnp.bfloat16


def rms_norm(act_in, gain_vec):
    act_f = act_in.astype(F32)
    inv_rms = lax.rsqrt(jnp.mean(act_f * act_f, axis=-1, keepdims=True) + RMS_EPS)
    return (act_f * inv_rms * gain_vec.astype(F32)).astype(BF16), inv_rms


def rms_norm_bwd(act_in, gain_vec, inv_rms, d_normed):
    act_f = act_in.astype(F32)
    d_f = d_normed.astype(F32)
    scaled_d = d_f * gain_vec.astype(F32)
    proj_mean = jnp.mean(scaled_d * act_f, axis=-1, keepdims=True)
    d_act = inv_rms * scaled_d - act_f * (inv_rms * inv_rms * inv_rms) * proj_mean
    d_gain = jnp.sum(d_f * act_f * inv_rms, axis=0)
    return d_act, d_gain


def dot(lhs, rhs, l_dim, r_dim):
    return lax.dot_general(lhs, rhs, (((l_dim,), (r_dim,)), ((), ())), preferred_element_type=F32)


def gather(shard):
    return lax.all_gather(shard, SEQ_AXIS, axis=0, tiled=True)


def exchange(blocks):
    return lax.all_to_all(blocks, SEQ_AXIS, 0, 0, tiled=True)


def rope_t(vals, cos_tab, sin_tab):
    half = vals.shape[0] // 2
    first, second = vals[:half], vals[half:]
    return jnp.concatenate([first * cos_tab - second * sin_tab, second * cos_tab + first * sin_tab], axis=0)


def mm(lhs, rhs):
    return jnp.dot(lhs, rhs, preferred_element_type=F32)


def diag_mask(tile):
    key_at = lax.broadcasted_iota(jnp.int32, (tile, tile), 0)
    query_at = lax.broadcasted_iota(jnp.int32, (tile, tile), 1)
    return key_at <= query_at


def attn_fwd_kernel(tile, q_t, k_ref, v_t, o_ref, of_ref, lse_ref, s_buf):
    step = pl.program_id(0)
    query = q_t[...]

    def scores(j):
        return mm(k_ref[pl.ds(pl.multiple_of(j * tile, tile), tile), :], query)

    def absorb(j, logits, top, total):
        new_top = jnp.maximum(top, jnp.max(logits, axis=0, keepdims=True))
        s_buf[pl.ds(pl.multiple_of(j * tile, tile), tile), :] = logits
        return new_top, total * jnp.exp(top - new_top) + jnp.sum(jnp.exp(logits - new_top), axis=0, keepdims=True)

    top, total = absorb(step, jnp.where(diag_mask(tile), scores(step), MASK_VALUE), jnp.full((1, tile), MASK_VALUE, F32), jnp.zeros((1, tile), F32))
    top, total = lax.fori_loop(0, step, lambda j, c: absorb(j, scores(j), *c), (top, total))
    lse = top + jnp.log(total)

    def weigh(j, acc):
        at = pl.ds(pl.multiple_of(j * tile, tile), tile)
        prob = jnp.exp(s_buf[at, :] - lse).astype(BF16)
        return acc + mm(v_t[:, at], prob)

    out = lax.fori_loop(0, step + 1, weigh, jnp.zeros((v_t.shape[0], tile), F32))
    of_ref[...] = out
    lse_ref[...] = lse
    block = o_ref.shape[2]
    for part in range(tile // block):
        o_ref[part] = out[:, part * block:(part + 1) * block].astype(BF16)


def attention_fwd(q_t, k_in, v_t, n_blocks):
    head_dim, seq = q_t.shape
    block = seq // n_blocks
    per = TILE // block
    return pl.pallas_call(
        lambda *refs: attn_fwd_kernel(TILE, *refs),
        grid=(seq // TILE,),
        in_specs=[pl.BlockSpec((head_dim, TILE), lambda i: (0, i)), pl.BlockSpec((seq, head_dim), lambda i: (0, 0)), pl.BlockSpec((head_dim, seq), lambda i: (0, 0))],
        out_specs=[pl.BlockSpec((per, head_dim, block), lambda i: (i, 0, 0)), pl.BlockSpec((head_dim, TILE), lambda i: (0, i)), pl.BlockSpec((1, TILE), lambda i: (0, i))],
        out_shape=[jax.ShapeDtypeStruct((n_blocks, head_dim, block), BF16), jax.ShapeDtypeStruct((head_dim, seq), F32), jax.ShapeDtypeStruct((1, seq), F32)],
        scratch_shapes=[pltpu.VMEM((seq, TILE), F32)],
        cost_estimate=pl.CostEstimate(flops=8 * seq * seq * head_dim, bytes_accessed=8 * seq * head_dim, transcendentals=seq * seq),
        name='attn_fwd',
    )(q_t, k_in, v_t)


def attn_bwd_kernel(tile, q_ref, q_t, do_ref, do_t, of_t, lse_ref, k_ref, k_t, v_ref, dq_t, dk_ref, dv_ref, acc):
    step = pl.program_id(0)
    query, query_t, d_out, d_out_t = q_ref[...], q_t[...], do_ref[...], do_t[...]
    lse = lse_ref[...]
    delta = jnp.sum(d_out_t.astype(F32) * of_t[...], axis=0, keepdims=True)

    @pl.when(step == 0)
    def _():
        dk_ref[...] = jnp.zeros_like(dk_ref)
        dv_ref[...] = jnp.zeros_like(dv_ref)

    acc[...] = jnp.zeros_like(acc)

    def visit(j, masked):
        at = pl.ds(pl.multiple_of(j * tile, tile), tile)
        logits = mm(k_ref[at, :], query_t)
        prob = jnp.exp(logits - lse)
        if masked:
            prob = jnp.where(diag_mask(tile), prob, 0.0)
        d_prob = mm(v_ref[at, :], d_out_t).astype(BF16).astype(F32)
        d_logits = (prob * (d_prob - delta)).astype(BF16)
        dv_ref[at, :] += mm(prob.astype(BF16), d_out)
        dk_ref[at, :] += mm(d_logits, query)
        acc[...] += mm(k_t[:, at], d_logits)

    visit(step, True)

    @pl.loop(0, step)
    def _(j):
        visit(j, False)

    dq_t[...] = acc[...]


def attention_bwd(q_in, q_t, do_in, do_t, of_t, lse, k_in, k_t, v_in):
    head_dim, seq = q_t.shape
    rows = pl.BlockSpec((TILE, head_dim), lambda i: (i, 0))
    cols = pl.BlockSpec((head_dim, TILE), lambda i: (0, i))
    all_rows = pl.BlockSpec((seq, head_dim), lambda i: (0, 0))
    all_cols = pl.BlockSpec((head_dim, seq), lambda i: (0, 0))
    return pl.pallas_call(
        lambda *refs: attn_bwd_kernel(TILE, *refs),
        grid=(seq // TILE,),
        in_specs=[rows, cols, rows, cols, cols, pl.BlockSpec((1, TILE), lambda i: (0, i)), all_rows, all_cols, all_rows],
        out_specs=[cols, all_rows, all_rows],
        out_shape=[jax.ShapeDtypeStruct((head_dim, seq), F32), jax.ShapeDtypeStruct((seq, head_dim), F32), jax.ShapeDtypeStruct((seq, head_dim), F32)],
        scratch_shapes=[pltpu.VMEM((head_dim, TILE), F32)],
        cost_estimate=pl.CostEstimate(flops=20 * seq * seq * head_dim, bytes_accessed=20 * seq * head_dim, transcendentals=seq * seq),
        name='attn_bwd',
    )(q_in, q_t, do_in, do_t, of_t, lse, k_in, k_t, v_in)


def gate_backward(d_mixed, gate_pre, up_pre):
    gate_sig = jax.nn.sigmoid(gate_pre)
    d_up = (d_mixed * gate_pre * gate_sig).astype(BF16)
    d_gate = (d_mixed * up_pre * gate_sig * (1.0 + gate_pre * (1.0 - gate_sig))).astype(BF16)
    return d_gate, d_up


def device_step(n_dev, x_act, positions, grad_out, g_attn_s, w_q, w_k, w_v, w_o, g_mlp_s, w_gate, w_up, w_down):
    tok, width = x_act.shape
    seq = tok * n_dev
    rows, heads, head_dim = w_q.shape
    ff = w_gate.shape[1]
    ff_s = ff // n_dev
    qkv = 3 * head_dim

    small = jnp.concatenate([(positions // 64).astype(BF16), (positions % 64).astype(BF16), g_attn_s, g_mlp_s])
    small = jnp.pad(small, (0, width - small.shape[0]))[None, :]
    x_ext = gather(jnp.concatenate([x_act, jnp.pad(small, ((0, 7), (0, 0)))], axis=0)[None])
    w_qkv = jnp.concatenate([w_q, w_k, w_v], axis=2)
    col_parts = jnp.concatenate([w_qkv, w_gate.reshape(rows, n_dev, ff_s), w_up.reshape(rows, n_dev, ff_s)], axis=2)
    w_cols = exchange(jnp.transpose(col_parts, (1, 0, 2))).reshape(width, qkv + 2 * ff_s)
    w_od = gather(jnp.concatenate([w_o[0], w_down], axis=0)[None])
    w_o_all = w_od[:, :head_dim].reshape(width, width)
    w_down_all = w_od[:, head_dim:].reshape(ff, width)
    w_gu = gather(jnp.concatenate([w_gate, w_up], axis=1))
    w_qkv_all = gather(w_qkv.reshape(rows, heads * qkv))

    x_all = x_ext[:, :tok].reshape(seq, width)
    extra = x_ext[:, tok].astype(F32)
    pos_all = extra[:, :tok] * 64.0 + extra[:, tok:2 * tok]
    g_attn = extra[:, 2 * tok:2 * tok + rows].reshape(width)
    g_mlp = extra[:, 2 * tok + rows:2 * tok + 2 * rows].reshape(width)
    half = head_dim // 2
    inv_freq = ROPE_BASE ** (-(jnp.arange(half, dtype=F32) * (2.0 / head_dim)))
    angle_t = inv_freq[:, None] * pos_all.reshape(1, seq)
    cos_t, sin_t = jnp.cos(angle_t), jnp.sin(angle_t)

    u_all = rms_norm(x_all, g_attn)[0]
    proj_t = dot(w_cols[:, :qkv], u_all, 0, 1)
    q_t = (rope_t(proj_t[:head_dim], cos_t, sin_t).astype(BF16).astype(F32) * (head_dim ** -0.5)).astype(BF16)
    k_t = rope_t(proj_t[head_dim:2 * head_dim], cos_t, sin_t).astype(BF16)
    v_t = proj_t[2 * head_dim:].astype(BF16)
    q_in, k_in, v_in = q_t.T, k_t.T, v_t.T
    o_blocks, of_t, lse = attention_fwd(q_t, k_in, v_t, n_dev)
    o_loc = exchange(o_blocks).reshape(width, tok)

    hidden = (x_act.astype(F32) + dot(o_loc, w_o_all, 0, 0)).astype(BF16)
    normed_mlp, inv_rms_mlp = rms_norm(hidden, g_mlp)
    a_dy = gather(jnp.concatenate([normed_mlp, grad_out], axis=1))
    pre = dot(normed_mlp, w_gu, 1, 0)
    gate_pre, up_pre = pre[:, :ff], pre[:, ff:]
    mixed = (jax.nn.silu(gate_pre) * up_pre).astype(BF16)
    y_out = (hidden.astype(F32) + dot(mixed, w_down_all, 1, 0)).astype(BF16)

    d_mixed = dot(grad_out, w_down_all, 1, 1).astype(BF16).astype(F32)
    d_gu = jnp.concatenate(gate_backward(d_mixed, gate_pre, up_pre), axis=1)
    d_normed = dot(d_gu, w_gu, 1, 1).astype(BF16)
    d_hid_norm, part_g_mlp = rms_norm_bwd(hidden, g_mlp, inv_rms_mlp, d_normed)
    d_hidden = (grad_out.astype(F32) + d_hid_norm).astype(BF16)
    do_blocks = exchange(dot(w_o_all, d_hidden, 1, 1).astype(BF16).reshape(n_dev, head_dim, tok))
    dh_all = gather(d_hidden)

    do_t = jnp.transpose(do_blocks, (1, 0, 2)).reshape(head_dim, seq)
    dq_t, dk, dv = attention_bwd(q_in, q_t, do_t.T, do_t, of_t, lse, k_in, k_t, v_in)
    dq_t = (dq_t * (head_dim ** -0.5)).astype(BF16).astype(F32)
    dk_t = dk.astype(BF16).T.astype(F32)
    d_proj_t = jnp.concatenate([rope_t(dq_t, cos_t, -sin_t).astype(BF16), rope_t(dk_t, cos_t, -sin_t).astype(BF16), dv.astype(BF16).T], axis=0)
    d_proj = exchange(jnp.transpose(d_proj_t.reshape(qkv, n_dev, tok), (1, 0, 2))).reshape(heads * qkv, tok)
    grad_w_qkv = dot(u_all, d_proj_t, 0, 1)

    inv_rms = lax.rsqrt(jnp.mean(jnp.square(x_act.astype(F32)), axis=-1, keepdims=True) + RMS_EPS)
    d_u = dot(d_proj, w_qkv_all, 0, 1).astype(BF16)
    d_x_norm, part_g_attn = rms_norm_bwd(x_act, g_attn, inv_rms, d_u)
    grad_x = (d_hidden.astype(F32) + d_x_norm).astype(BF16)

    a_all, dy_all = a_dy[:, :width], a_dy[:, width:]
    pre_t = dot(w_cols[:, qkv:], a_all, 0, 1)
    gate_t, up_t = pre_t[:ff_s], pre_t[ff_s:]
    d_mixed_t = dot(w_down, dy_all, 1, 1).astype(BF16).astype(F32)
    mixed_t = (jax.nn.silu(gate_t) * up_t).astype(BF16)
    d_gu_t = jnp.concatenate(gate_backward(d_mixed_t, gate_t, up_t), axis=0)
    grad_w_down = dot(mixed_t, dy_all, 1, 0)
    grad_w_gu = dot(a_all, d_gu_t, 0, 1)
    grad_w_o = dot(o_blocks.transpose(1, 0, 2).reshape(head_dim, seq), dh_all, 1, 0)[None]

    mlp_back = exchange(jnp.concatenate([grad_w_gu, part_g_mlp[:, None]], axis=1).reshape(n_dev, rows, 2 * ff_s + 1))
    attn_back = exchange(jnp.concatenate([grad_w_qkv, part_g_attn[:, None]], axis=1).reshape(n_dev, rows, qkv + 1))
    grad_g_mlp = jnp.sum(mlp_back[:, :, 2 * ff_s], axis=0)
    grad_g_attn = jnp.sum(attn_back[:, :, qkv], axis=0)
    mlp_rows = jnp.transpose(mlp_back, (1, 0, 2))
    attn_rows = jnp.transpose(attn_back, (1, 0, 2))
    grad_w_gate = mlp_rows[:, :, :ff_s].reshape(rows, ff)
    grad_w_up = mlp_rows[:, :, ff_s:2 * ff_s].reshape(rows, ff)
    grad_w_q, grad_w_k, grad_w_v = (attn_rows[:, :, i * head_dim:(i + 1) * head_dim] for i in range(3))
    return (y_out, grad_x, grad_g_attn, grad_w_q, grad_w_k, grad_w_v, grad_w_o, grad_g_mlp, grad_w_gate, grad_w_up, grad_w_down)


def solution(mesh):
    n_dev = mesh.shape[SEQ_AXIS]
    token_spec = P(SEQ_AXIS, None)
    cube_spec = P(SEQ_AXIS, None, None)
    gain_spec = P(SEQ_AXIS)
    weight_specs = (gain_spec, cube_spec, cube_spec, cube_spec, cube_spec, gain_spec, token_spec, token_spec, token_spec)
    return jax.shard_map(lambda *args: device_step(n_dev, *args), mesh=mesh, in_specs=(token_spec, gain_spec, token_spec) + weight_specs, out_specs=(token_spec, token_spec) + weight_specs, check_vma=False)
```

time: 1460 us -> 432 us (0.30)
  waiting for transfers between devices: 790 us -> 127 us
  matrix products: 302 us -> 79.5 us
  blocking collectives: 113 us -> 0 us
  Pallas kernels: 0 us -> 62.8 us
  other arithmetic: 108 us -> 51.5 us
    reduce_scatter x7 -> x0, waiting for transfers between devices: 541 us -> none  [device_step(): lax.psum_scatter(full_grad, SEQ_AXIS, scatter_dimension=0, tiled=True)]
    dot_general x28 -> x14, matrix products: 294 us -> 79.5 us  [dot(): lax.dot_general(lhs, rhs, (((l_dim,), (r_dim,)), ((), ())), preferred_ele...]
    all_gather x14 -> x6, waiting for transfers between devices: 163 us -> 52.3 us  [gather(): return lax.all_gather(shard, SEQ_AXIS, axis=0, tiled=True)]
    unnamed x3 -> x0, blocking collectives: 99.3 us -> none
    pallas_call x0 -> x2, Pallas kernels: none -> 62.8 us  [the longest x1 32.2 us: attention_bwd(): pl.pallas_call(lambda *refs: attn_bwd_kernel(TILE, *refs), grid=(seq // T...]
    reduce_sum x2 -> x3, other arithmetic: 43.5 us -> 1.81 us  [the longest x1 0.81 us: device_step(): grad_g_attn = jnp.sum(attn_back[:, :, qkv], axis=0)]
    another operation x4 -> x2, other arithmetic: 46 us -> 5.51 us
    all_gather x7 -> x0, local copies, waits for them, and re-layouts: 35.8 us -> none  [gather_weights(): lax.all_gather(shard_part, SEQ_AXIS, axis=0, tiled=True)]
  transfers between devices with their start and end apart: 32 -> 12, of which waited for: 19 -> 8; matrix products, arithmetic and copies ran while one was open for 29% -> 44% of each run, Pallas kernels for 0% -> 15%
where the time goes in v1:
time: 432 us; the launch traced here: 427 us
  waiting for transfers between devices  127 us (29%)
  matrix products  79.5 us (18%)
  local copies, waits for them, and re-layouts  72 us (17%)
  Pallas kernels  62.8 us (15%)
  other arithmetic  51.5 us (12%)
  starting transfers between devices  19.6 us (5%)
  between operations  14.9 us (3%)
    dot_general x14, matrix products, dot(): lax.dot_general(lhs, rhs, (((l_dim,), (r_dim,)), ((), ())), preferred_ele...  79.5 us
    all_to_all x6, waiting for transfers between devices, exchange(): return lax.all_to_all(blocks, SEQ_AXIS, 0, 0, tiled=True)  74.2 us
    all_gather x6, waiting for transfers between devices, gather(): return lax.all_gather(shard, SEQ_AXIS, axis=0, tiled=True)  52.3 us
    pallas_call x1, Pallas kernels, attention_bwd(): pl.pallas_call(lambda *refs: attn_bwd_kernel(TILE, *refs), grid=(seq // T...  32.2 us
    pallas_call x1, Pallas kernels, attention_fwd(): pl.pallas_call(lambda *refs: attn_fwd_kernel(TILE, *refs), grid=(seq // T...  30.6 us
    all_to_all x6, starting transfers between devices, exchange(): return lax.all_to_all(blocks, SEQ_AXIS, 0, 0, tiled=True)  18.9 us
    convert_element_type x1, local copies, waits for them, and re-layouts, rms_norm(): act_f = act_in.astype(F32)  17.5 us
    convert_element_type x1, other arithmetic, rms_norm(): act_f = act_in.astype(F32)  11.3 us
  transfers between devices with their start and end apart: 12, of which 8 were waited for; matrix products, arithmetic and copies ran while one was open for 44% of the time, Pallas kernels for 15%

profile of v1, /device:TPU:0, one launch (start us, length us, event | category | flops | bytes accessed | tf_op | source)
XLA Modules:
  0.0 427.1 jit_solution(232557690588132177)
XLA Ops:
  20.1 5.6 %all-to-all-start = ((bf16[16,64,544]{2,1,0:T(8,128)(2,1)}), bf16[16,64,544]{2,1,0:T(8,128)(2,1)S(1)}, u32[]{:S(2)}, u32[]{:S(2)}) async-start(bf16[16,64,544]{2,1,0:T(8,128)(2,1)} %bitcast), calls=%async_computation | async-start | bytes 2621440 | tf_op jit(solution)/shard_map/all_to_all | solution.py:42
  25.7 48.3 %all-gather.17.cloned.1.call-done = bf16[4224,1024]{1,0:T(8,128)(2,1)} async-done(((bf16[264,1024]{1,0:T(8,128)(2,1)}), bf16[4224,1024]{1,0:T(8,128)(2,1)}) %all-gather.17.cloned.1.call-update) | async-done | bytes 8650768 | tf_op jit(solution)/shard_map/all_gather | solution.py:38
  75.1 11.3 %slice_convert_fusion = f32[16,256,1024]{2,1,0:T(8,128)} fusion(bf16[16,264,1024]{2,1,0:T(8,128)(2,1)} %bitcast.78), kind=kLoop, calls=%fused_computation.2 | loop fusion | flops 4194304 | bytes 25165824 | tf_op jit(solution)/shard_map/convert_element_type | solution.py:18
  86.5 17.5 %copy.135 = f32[4096,1024]{0,1:T(8,128)} copy(f32[4096,1024]{1,0:T(8,128)} %bitcast.75) | data formatting | bytes 33554432 | tf_op jit(solution)/shard_map/convert_element_type | solution.py:18
  103.9 5.1 %multiply_reduce_fusion = f32[16,256]{1,0:T(8,128)S(1)} fusion(bf16[16,264,1024]{2,1,0:T(8,128)(2,1)} %bitcast.79), kind=kLoop, calls=%fused_computation.1 | loop fusion | flops 12578816 | bytes 8404992 | tf_op jit(solution)/shard_map/reduce_sum | solution.py:19
  109.1 9.7 %multiply_convert_fusion = bf16[4096,1024]{0,1:T(8,128)(2,1)} fusion(f32[4096,1024]{0,1:T(8,128)} %copy.135, f32[1024]{0:T(1024)S(1)} %mul.297, f32[4096]{0:T(1024)S(1)} %bitcast.106), kind=kLoop, calls=%fused_computation | loop fusion | flops 12582912 | bytes 25186304 | tf_op jit(solution)/shard_map/convert_element_type | solution.py:20
  118.7 5.8 %fusion.92 = f32[192,4096]{1,0:T(8,128)S(1)} fusion(bf16[4096,1024]{0,1:T(8,128)(2,1)} %multiply_convert_fusion, bf16[1024,544]{1,0:T(8,128)(2,1)S(1)} %bitcast.92), kind=kOutput, calls=%fused_computation.127 | convolution fusion | flops 1610612736 | bytes 12058624 | tf_op jit(solution)/shard_map/dot_general | solution.py:34
  131.1 30.6 %attn_fwd.1 = (bf16[16,64,256]{2,1,0:T(8,128)(2,1)}, f32[64,4096]{1,0:T(8,128)}, f32[1,4096]{1,0:T(1,128)}) custom-call(bf16[64,4096]{1,0:T(8,128)(2,1)} %get-tuple-element.102.refs_0_.refs_1_, bf16[4096,64]{1,0:T(8,128)(2,1)} %copy.137.refs_1_.refs_6_, bf16[64,4096]{1,0:T(8,128)(2,1)} %slice.238.refs_2_), custom_call_target="tpu_custom_call" | custom-call | flops 8589934592 | bytes 2097152 | tf_op jit(solution)/shard_map/attn_fwd/pallas_call | solution.py:94
  164.3 16.2 %all-to-all-done.1 = bf16[16,64,256]{2,1,0:T(8,128)(2,1)S(1)} async-done(((bf16[16,64,256]{2,1,0:T(8,128)(2,1)}), bf16[16,64,256]{2,1,0:T(8,128)(2,1)S(1)}, u32[]{:S(2)}, u32[]{:S(2)}) %all-to-all-start.1) | async-done | bytes 524320 | tf_op jit(solution)/shard_map/all_to_all | solution.py:42
  184.9 6.0 %slice.150 = bf16[16,176,1024]{2,1,0:T(8,128)(2,1)} slice(bf16[16,240,1024]{2,1,0:T(8,128)(2,1)} %bitcast.86), slice={[0:16], [64:240], [0:1024]} | slice | bytes 11534336 | tf_op jit(solution)/shard_map/slice | solution.py:181
  191.1 6.1 %fusion.114 = f32[256,5632]{1,0:T(8,128)S(1)} fusion(bf16[256,1024]{1,0:T(8,128)(2,1)S(1)} %fusion.51, bf16[1024,5632]{1,0:T(8,128)(2,1)} %all-gather.9.cloned.1.call-done), kind=kOutput, calls=%fused_computation.172 | convolution fusion | flops 2952790016 | bytes 17825792 | tf_op jit(solution)/shard_map/dot_general | solution.py:34
  203.8 5.8 %fusion.55 = (f32[1024]{0:T(1024)S(1)}, f32[256]{0:T(256)S(1)}, bf16[256,1024]{1,0:T(8,128)(2,1)}) fusion(bf16[256,1024]{1,0:T(8,128)(2,1)S(1)} %get-tuple-element.114, f32[256]{0:T(256)S(1)} %get-tuple-element.110, f32[1024]{0:T(1024)S(1)} %mul.320, bf16[1024,5632]{1,0:T(8,128)(2,1)S(1)} %bitcast.81, bf16[256,2816]{1,0:T(8,128)(2,1)} %get-tuple-element.85, ...), kind=kOutput, calls=%fused_computation.78 | convolution fusion | flops 2960915200 | bytes 15476736 | tf_op jit(solution)/shard_map/dot_general | solution.py:34
  220.8 12.6 %all-to-all-done.2 = bf16[16,64,256]{2,1,0:T(8,128)(2,1)S(1)} async-done(((bf16[16,64,256]{2,1,0:T(8,128)(2,1)}), bf16[16,64,256]{2,1,0:T(8,128)(2,1)S(1)}, u32[]{:S(2)}, u32[]{:S(2)}) %all-to-all-start.2) | async-done | bytes 524320 | tf_op jit(solution)/shard_map/all_to_all | solution.py:42
  234.9 32.2 %attn_bwd.1 = (f32[64,4096]{1,0:T(8,128)}, f32[4096,64]{1,0:T(8,128)}, f32[4096,64]{1,0:T(8,128)}) custom-call(bf16[4096,64]{1,0:T(8,128)(2,1)} %copy.141.refs_0_, bf16[64,4096]{1,0:T(8,128)(2,1)} %get-tuple-element.102.refs_0_.refs_1_, bf16[4096,64]{1,0:T(8,128)(2,1)} %copy.142.refs_2_, bf16[64,4096]{1,0:T(8,128)(2,1)} %bitcast.95, ...), custom_call_target="tpu_custom_call" | custom-call | flops 21474836480 | bytes 5242880 | tf_op jit(solution)/shard_map/attn_bwd/pallas_call | solution.py:146
  281.8 5.8 %concatenate.66 = bf16[192,4096]{0,1:T(8,128)(2,1)S(1)} concatenate(bf16[32,4096]{0,1:T(8,128)(2,1)} %copy.145, bf16[32,4096]{0,1:T(8,128)(2,1)} %copy.146, bf16[32,4096]{0,1:T(8,128)(2,1)} %copy.147, bf16[32,4096]{0,1:T(8,128)(2,1)} %copy.148, bf16[64,4096]{0,1:T(8,128)(2,1)} %convert_bitcast_fusion.1), dimensions={0} | concatenate | bytes 3145728 | tf_op jit(solution)/shard_map/concatenate | solution.py:224
  295.1 6.7 %fusion.26 = f32[16,64,192]{2,1,0:T(8,128)} fusion(bf16[16,64,4096]{2,1,0:T(8,128)(2,1)} %bitcast.76, bf16[192,4096]{0,1:T(8,128)(2,1)S(1)} %concatenate.66), kind=kOutput, calls=%fused_computation.38 | convolution fusion | flops 1610612736 | bytes 10747904 | tf_op jit(solution)/shard_map/dot_general | solution.py:34
  301.8 29.9 %all-to-all-done.3 = bf16[16,192,256]{2,1,0:T(8,128)(2,1)} async-done(((bf16[16,192,256]{2,1,0:T(8,128)(2,1)}), bf16[16,192,256]{2,1,0:T(8,128)(2,1)}, u32[]{:S(2)}, u32[]{:S(2)}) %all-to-all-start.3) | async-done | bytes 1572896 | tf_op jit(solution)/shard_map/all_to_all | solution.py:42
  331.8 6.1 %fusion.48 = (f32[1024]{0:T(1024)S(1)}, f32[256]{0:T(256)S(1)}, bf16[256,1024]{1,0:T(8,128)(2,1)}) fusion(bf16[256,1024]{1,0:T(8,128)(2,1)S(1)} %copy-done.3, f32[256]{0:T(256)S(1)} %get-tuple-element.108, f32[1024]{0:T(1024)S(1)} %mul.297, bf16[3072,256]{1,0:T(8,128)(2,1)} %bitcast.20, bf16[1024,3072]{1,0:T(8,128)(2,1)} %all-gather.11.cloned.1.call-done), kind=kOutput, calls=%fused_computation.71 | convolution fusion | flops 1612970752 | bytes 8923136 | tf_op jit(solution)/shard_map/dot_general | solution.py:34
  342.1 6.9 %fusion.30 = bf16[256,1024]{1,0:T(8,128)(2,1)} fusion(bf16[2816,1024]{1,0:T(8,128)(2,1)} %bitcast.89, f32[256,5632]{1,0:T(8,128)} %copy-done.1, bf16[256,1024]{1,0:T(8,128)(2,1)S(1)} %copy-done.8), kind=kOutput, calls=%fused_computation.51 | convolution fusion | flops 1481506816 | bytes 12582912 | tf_op jit(solution)/shard_map/dot_general | solution.py:34
  351.3 10.5 %all-to-all-done.4 = f32[16,64,193]{2,1,0:T(8,128)S(1)} async-done(((f32[16,64,193]{2,1,0:T(8,128)}), f32[16,64,193]{2,1,0:T(8,128)S(1)}, u32[]{:S(2)}, u32[]{:S(2)}) %all-to-all-start.4) | async-done | bytes 790560 | tf_op jit(solution)/shard_map/all_to_all | solution.py:42
  366.2 9.8 %fusion.6 = f32[352,4096]{1,0:T(8,128)} fusion(bf16[4096,2048]{1,0:T(8,128)(2,1)} %all-gather.15.cloned.1.call-done, bf16[1024,544]{1,0:T(8,128)(2,1)S(1)} %bitcast.93), kind=kOutput, calls=%fused_computation.9 | convolution fusion | flops 2952790016 | bytes 14942208 | tf_op jit(solution)/shard_map/dot_general | solution.py:34
  376.1 5.9 %multiply_convert_fusion.3 = (bf16[176,4096]{1,0:T(8,128)(2,1)S(1)}, bf16[176,4096]{1,0:T(8,128)(2,1)S(1)}) fusion(f32[352,4096]{1,0:T(8,128)} %fusion.6, bf16[176,1024]{1,0:T(8,128)(2,1)S(1)} %copy-done.24, bf16[4096,2048]{1,0:T(8,128)(2,1)S(1)} %copy-done.25), kind=kOutput, calls=%fused_computation.26 | convolution fusion | flops 1487208448 | bytes 17399808 | tf_op jit(solution)/shard_map/dot_general | solution.py:34
  394.2 5.7 %convolution_bitcast_fusion.1 = f32[1,64,1024]{2,1,0:T(8,128)} fusion(bf16[64,4096]{1,0:T(8,128)(2,1)S(1)} %bitcast.91, bf16[4096,1024]{1,0:T(8,128)(2,1)} %all-gather.13.cloned.1.call-done), kind=kOutput, calls=%fused_computation.58 | convolution fusion | flops 536870912 | bytes 9175040 | tf_op jit(solution)/shard_map/dot_general | solution.py:34
  399.9 7.7 %fusion = f32[176,1024]{1,0:T(8,128)} fusion(bf16[4096,2048]{1,0:T(8,128)(2,1)} %all-gather.15.cloned.1.call-done, f32[352,4096]{1,0:T(8,128)} %fusion.6), kind=kOutput, calls=%fused_computation.3 | convolution fusion | flops 1480720384 | bytes 14876672 | tf_op jit(solution)/shard_map/dot_general | solution.py:34
  (158 shorter events, 104.3 us)
Async XLA Ops:
  7.2 6.5 %copy-start.18 = (bf16[64,16,64]{2,1,0:T(8,128)(2,1)S(1)}, bf16[64,16,64]{2,1,0:T(8,128)(2,1)}, u32[]{:S(2)}) copy-start(bf16[64,16,64]{2,1,0:T(8,128)(2,1)} %param.16) | copy-start | bytes 393220
  7.2 6.5 %copy-start.19 = (bf16[64,16,64]{2,1,0:T(8,128)(2,1)S(1)}, bf16[64,16,64]{2,1,0:T(8,128)(2,1)}, u32[]{:S(2)}) copy-start(bf16[64,16,64]{2,1,0:T(8,128)(2,1)} %param.17) | copy-start | bytes 393220
  7.2 66.7 %all-gather.17.cloned.1.call-start = ((), (), s32[]{:S(2)}) async-start(), calls=%async_computation.10 | async-start | bytes 9191424 | tf_op jit(solution)/shard_map/all_gather | solution.py:38
  10.7 153.6 %all-gather.19.cloned.1.call-start = ((), (), s32[]{:S(2)}) async-start(), calls=%async_computation.11 | async-start | bytes 8355840 | tf_op jit(solution)/shard_map/all_gather | solution.py:38
  12.6 178.5 %all-gather.9.cloned.1.call-start = ((), (), s32[]{:S(2)}) async-start(), calls=%async_computation.6 | async-start | bytes 12255232 | tf_op jit(solution)/shard_map/all_gather | solution.py:38
  13.6 288.2 %all-gather.11.cloned.1.call-start = ((), (), s32[]{:S(2)}) async-start(), calls=%async_computation.7 | async-start | bytes 6684672 | tf_op jit(solution)/shard_map/all_gather | solution.py:38
  20.1 98.6 %all-to-all-start = ((bf16[16,64,544]{2,1,0:T(8,128)(2,1)}), bf16[16,64,544]{2,1,0:T(8,128)(2,1)S(1)}, u32[]{:S(2)}, u32[]{:S(2)}) async-start(bf16[16,64,544]{2,1,0:T(8,128)(2,1)} %bitcast), calls=%async_computation | async-start | bytes 2621440 | tf_op jit(solution)/shard_map/all_to_all | solution.py:42
  131.1 49.4 %copy-start.3 = (bf16[256,1024]{1,0:T(8,128)(2,1)S(1)}, bf16[256,1024]{1,0:T(8,128)(2,1)}, u32[]{:S(2)}) copy-start(bf16[256,1024]{1,0:T(8,128)(2,1)} %param.12) | copy-start | bytes 1572868
  161.7 18.8 %all-to-all-start.1 = ((bf16[16,64,256]{2,1,0:T(8,128)(2,1)}), bf16[16,64,256]{2,1,0:T(8,128)(2,1)S(1)}, u32[]{:S(2)}, u32[]{:S(2)}) async-start(bf16[16,64,256]{2,1,0:T(8,128)(2,1)} %get-tuple-element.17), calls=%async_computation.1 | async-start | bytes 1048576 | tf_op jit(solution)/shard_map/all_to_all | solution.py:42
  164.2 19.0 %copy-start.14 = (bf16[256,1024]{1,0:T(8,128)(2,1)S(1)}, bf16[256,1024]{1,0:T(8,128)(2,1)}, u32[]{:S(2)}) copy-start(bf16[256,1024]{1,0:T(8,128)(2,1)} %param.14) | copy-start | bytes 1572868
  164.2 202.0 %all-gather.15.cloned.1.call-start = ((), (), s32[]{:S(2)}) async-start(), calls=%async_computation.9 | async-start | bytes 17825792 | tf_op jit(solution)/shard_map/all_gather | solution.py:38
  182.9 26.8 %copy-start.7 = (bf16[256,1024]{1,0:T(8,128)(2,1)}, bf16[256,1024]{1,0:T(8,128)(2,1)S(1)}, u32[]{:S(2)}) copy-start(bf16[256,1024]{1,0:T(8,128)(2,1)S(1)} %get-tuple-element.114) | copy-start | bytes 1572868
  184.3 209.9 %all-gather.13.cloned.1.call-start = ((), (), s32[]{:S(2)}) async-start(), calls=%async_computation.8 | async-start | bytes 8912896 | tf_op jit(solution)/shard_map/all_gather | solution.py:38
  191.1 10.6 %slice-start = ((s8[11534336]{0:T(1024)(128)(4,1)}), s8[4194304]{0:T(1024)(128)(4,1)S(1)}, s32[]{:S(2)}) async-start(s8[11534336]{0:T(1024)(128)(4,1)} %bitcast.80), calls=%async_computation.12 | async-start | bytes 8388608
  197.3 6.5 %slice-start.2 = ((s8[11534336]{0:T(1024)(128)(4,1)}), s8[3145728]{0:T(1024)(128)(4,1)S(1)}, s32[]{:S(2)}) async-start(s8[11534336]{0:T(1024)(128)(4,1)} %bitcast.80), calls=%async_computation.14 | async-start | bytes 6291456
  215.5 18.0 %all-to-all-start.2 = ((bf16[16,64,256]{2,1,0:T(8,128)(2,1)}), bf16[16,64,256]{2,1,0:T(8,128)(2,1)S(1)}, u32[]{:S(2)}, u32[]{:S(2)}) async-start(bf16[16,64,256]{2,1,0:T(8,128)(2,1)} %bitcast.12), calls=%async_computation.2 | async-start | bytes 1048576 | tf_op jit(solution)/shard_map/all_to_all | solution.py:42
  272.4 8.3 %copy-start.13 = (f32[4096,64]{1,0:T(8,128)S(1)}, f32[4096,64]{1,0:T(8,128)}, u32[]{:S(2)}) copy-start(f32[4096,64]{1,0:T(8,128)} %get-tuple-element.22) | copy-start | bytes 3145732
  289.9 41.8 %all-to-all-start.3 = ((bf16[16,192,256]{2,1,0:T(8,128)(2,1)}), bf16[16,192,256]{2,1,0:T(8,128)(2,1)}, u32[]{:S(2)}, u32[]{:S(2)}) async-start(bf16[16,192,256]{2,1,0:T(8,128)(2,1)} %bitcast.88), calls=%async_computation.3 | async-start | bytes 3145728 | tf_op jit(solution)/shard_map/all_to_all | solution.py:42
  339.4 22.4 %all-to-all-start.4 = ((f32[16,64,193]{2,1,0:T(8,128)}), f32[16,64,193]{2,1,0:T(8,128)S(1)}, u32[]{:S(2)}, u32[]{:S(2)}) async-start(f32[16,64,193]{2,1,0:T(8,128)} %pad_maximum_fusion.1), calls=%async_computation.4 | async-start | bytes 2097152 | tf_op jit(solution)/shard_map/all_to_all | solution.py:42
  342.1 8.1 %copy-start.23 = (bf16[256,1024]{1,0:T(8,128)(2,1)S(1)}, bf16[256,1024]{1,0:T(8,128)(2,1)}, u32[]{:S(2)}) copy-start(bf16[256,1024]{1,0:T(8,128)(2,1)} %get-tuple-element.116) | copy-start | bytes 1572868
  366.2 9.9 %copy-start.24 = (bf16[176,1024]{1,0:T(8,128)(2,1)S(1)}, bf16[176,1024]{1,0:T(8,128)(2,1)}, u32[]{:S(2)}) copy-start(bf16[176,1024]{1,0:T(8,128)(2,1)} %param.23) | copy-start | bytes 1081348
  366.2 9.9 %copy-start.25 = (bf16[4096,2048]{1,0:T(8,128)(2,1)S(1)}, bf16[4096,2048]{1,0:T(8,128)(2,1)}, u32[]{:S(2)}) copy-start(bf16[4096,2048]{1,0:T(8,128)(2,1)} %all-gather.15.cloned.1.call-done) | copy-start | bytes 50331652
  386.5 7.7 %copy-start.4 = (bf16[16,8,8,256]{3,2,0,1:T(8,128)(2,1)S(1)}, bf16[16,8,8,256]{3,2,0,1:T(8,128)(2,1)}, u32[]{:S(2)}) copy-start(bf16[16,8,8,256]{3,2,0,1:T(8,128)(2,1)} %copy.167) | copy-start | bytes 1572868
  388.0 24.6 %all-to-all-start.5 = ((f32[16,64,353]{2,1,0:T(8,128)}), f32[16,64,353]{2,1,0:T(8,128)S(1)}, u32[]{:S(2)}, u32[]{:S(2)}) async-start(f32[16,64,353]{2,1,0:T(8,128)} %pad_maximum_fusion), calls=%async_computation.5 | async-start | bytes 3145728 | tf_op jit(solution)/shard_map/all_to_all | solution.py:42
  (17 other events, 80.4 us)
Sparse Core Ops, SparseCore 0:
  10.8 63.0 all-gather.16
  76.8 46.8 all-gather.18
  126.5 64.5 all-gather.8
  193.2 46.1 all-gather.10
  241.6 92.9 all-gather.14
  337.2 56.9 all-gather.12
